TPU v7x, 32 devices: a whole 2x2x4 slice. The times are simulated.
32 devices in a mesh: groups: 2 (over x), frame: 16 (over z, y, core).
Axes of the slice: x: 2, y: 2, z: 4, core: 2. Of those that a mesh axis runs over, the one named last changes fastest.
Arguments:
- latents: bfloat16 [128, 2, 64, 320], P(('groups', 'frame')), parts along dimension 0, may hold values from -6 to 6
- norm_gain: float32 [320], replicated, may hold values from 0.1 to 1.9
- w_qkv: bfloat16 [320, 960], replicated, may hold values from -0.3125 to 0.3125
- w_out: bfloat16 [320, 320], replicated, may hold values from -0.3125 to 0.3125
- gn_gain: float32 [2, 320], replicated, may hold values from 0.1 to 1.9
- conv_one: bfloat16 [3, 3, 320, 320], replicated, may hold values from -0.109375 to 0.109375
- conv_two: bfloat16 [3, 3, 320, 320], replicated, may hold values from -0.109375 to 0.109375
- step_embed: float32 [320], replicated, may hold values from -4 to 4
- offsets: int32 [32], P('groups'), parts along dimension 0, may hold values from 0 to 3
- numerators: int32 [16], replicated, may hold values from 1 to 16
Outputs:
- result: bfloat16 [128, 2, 64, 320], P(('groups', 'frame')), parts along dimension 0
There are 2 independent parts, one for each index of `groups`. A program takes and returns all parts, laid end to end along the dimension named above; an argument that names none is the same for every part. Nothing has to cross between parts.
All inputs are finite; a program needn't handle non-finite values.
Results may differ from a plain program's by a relative error of at most 0.009.
Values may be sent and summed in bfloat16 or wider, within the bound.
A program may use at most 64 MiB of HBM per device.

v0:
```python
import jax
import jax.numpy as jnp
from jax import lax
from jax.sharding import PartitionSpec as P

HEADS = 5
HEAD_DIM = 64
NORM_GROUPS = 32
BLOCK = 4
WINDOW = 16


def shifted(shard, axis, by):
    count = lax.axis_size(axis)
    return lax.ppermute(shard, axis, [(i, (i + by) % count) for i in range(count)])


def layer_project(frames, norm_gain, w_qkv):
    channels = frames.shape[-1]
    values32 = frames.astype(jnp.float32)
    average = jnp.mean(values32, axis=-1, keepdims=True)
    centered = values32 - average
    variance = jnp.mean(centered * centered, axis=-1, keepdims=True)
    normed = (centered * lax.rsqrt(variance + 1e-05) * norm_gain).astype(jnp.bfloat16)
    qkv = jnp.dot(normed.reshape(-1, channels), w_qkv, preferred_element_type=jnp.float32).astype(
        jnp.bfloat16
    )
    return qkv.reshape(frames.shape[0], -1, 3 * channels)


def window_attend(window, numer_f):
    frame_count, pos_count, triple = window.shape
    channels = triple // 3
    queries = window[..., :channels].reshape(frame_count, pos_count, HEADS, HEAD_DIM)
    keys = window[..., channels : 2 * channels].reshape(frame_count, pos_count, HEADS, HEAD_DIM)
    values = window[..., 2 * channels :].reshape(frame_count, pos_count, HEADS, HEAD_DIM)
    scores = jnp.einsum(
        "jphd,kphd->phjk", queries, keys, preferred_element_type=jnp.float32
    ) / jnp.sqrt(jnp.float32(HEAD_DIM))
    highest = jnp.max(scores, axis=-1, keepdims=True)
    expos = jnp.exp(scores - highest)
    probs = (expos / jnp.sum(expos, axis=-1, keepdims=True)).astype(jnp.bfloat16)
    attended = jnp.einsum(
        "phjk,kphd->jphd", probs, values, preferred_element_type=jnp.float32
    ).reshape(frame_count, pos_count, channels)
    return (attended * numer_f[:, None, None]).astype(jnp.bfloat16)


def group_act(tensor, gain):
    shape = tensor.shape
    grouped = tensor.reshape(shape[0], shape[1], shape[2], NORM_GROUPS, shape[3] // NORM_GROUPS)
    average = jnp.mean(grouped, axis=(1, 2, 4), keepdims=True)
    centered = grouped - average
    variance = jnp.mean(centered * centered, axis=(1, 2, 4), keepdims=True)
    normed = (centered * lax.rsqrt(variance + 1e-05)).reshape(shape) * gain
    return jax.nn.silu(normed).astype(jnp.bfloat16)


def conv_three(tensor, kernel):
    return lax.conv_general_dilated(
        tensor,
        kernel,
        (1, 1),
        "SAME",
        dimension_numbers=("NHWC", "HWIO", "NHWC"),
        preferred_element_type=jnp.float32,
    )


def body(
    latents, norm_gain, w_qkv, w_out, gn_gain, conv_one, conv_two, step_embed, offsets, numerators
):
    block_len, tile_rows, tile_cols, channels = latents.shape
    reach = WINDOW // BLOCK
    nblocks = offsets.shape[0]
    position = lax.axis_index("frame")
    numer_f = numerators.astype(jnp.float32)
    pieces = [latents]
    for distance in range(1, reach + 1):
        pieces.append(shifted(latents, "frame", -distance))
    span = jnp.concatenate(pieces, 0)
    span = layer_project(span, norm_gain, w_qkv)
    block_ids = jnp.arange(nblocks, dtype=jnp.int32)
    start_shift = jnp.sum(jnp.where(block_ids == position, offsets, 0))
    window = lax.dynamic_slice_in_dim(span, start_shift, WINDOW, 0)
    weighted = window_attend(window, numer_f)
    pos_count = weighted.shape[1]
    slots = jnp.zeros(((reach + 1) * block_len, pos_count, channels), jnp.bfloat16)
    slots = lax.dynamic_update_slice_in_dim(slots, weighted, start_shift, 0)
    totals = slots[:block_len].astype(jnp.float32)
    for distance in range(1, reach + 1):
        piece = slots[distance * block_len : (distance + 1) * block_len]
        totals = totals + shifted(piece, "frame", distance).astype(jnp.float32)
    back_steps = jnp.arange(reach + 1, dtype=jnp.int32)
    owners = (position - back_steps) % nblocks
    shifts_back = jnp.sum(
        jnp.where(block_ids[None, :] == owners[:, None], offsets[None, :], 0), axis=1
    )
    slot_pos = (
        block_len * back_steps[:, None]
        + jnp.arange(block_len, dtype=jnp.int32)[None, :]
        - shifts_back[:, None]
    )
    matches = slot_pos[:, :, None] == jnp.arange(WINDOW, dtype=jnp.int32)[None, None, :]
    denominator = jnp.sum(jnp.where(matches, numer_f[None, None, :], 0.0), axis=(0, 2))
    combined = (totals / denominator[:, None, None]).astype(jnp.bfloat16)
    projected = jnp.dot(
        combined.reshape(-1, channels), w_out, preferred_element_type=jnp.float32
    ).reshape(latents.shape)
    hidden = (latents.astype(jnp.float32) + projected).astype(jnp.bfloat16)
    first_act = group_act(hidden.astype(jnp.float32), gn_gain[0])
    middle = conv_three(first_act, conv_one) + step_embed
    second_act = group_act(middle, gn_gain[1])
    return (hidden.astype(jnp.float32) + conv_three(second_act, conv_two)).astype(jnp.bfloat16)


def solution(mesh):
    return jax.shard_map(
        body,
        mesh=mesh,
        in_specs=(
            P(("groups", "frame"), None, None, None),
            P(),
            P(),
            P(),
            P(),
            P(),
            P(),
            P(),
            P("groups"),
            P(),
        ),
        out_specs=P(("groups", "frame"), None, None, None),
        check_vma=False,
    )
```

profile of v0, /device:TPU:5, one launch (start us, length us, event | category | flops | bytes accessed | tf_op | source)
XLA Modules:
  0.0 157.0 jit_solution(2478372511884069237)
XLA Ops:
  0.0 0.7 collective-permute-start
  0.7 4.7 %collective-permute-start.2 = (bf16[4,2,64,320]{3,2,1,0:T(8,128)(2,1)}, bf16[4,2,64,320]{3,2,1,0:T(8,128)(2,1)S(1)}, u32[]{:S(2)}, u32[]{:S(2)}) collective-permute-start(bf16[4,2,64,320]{3,2,1,0:T(8,128)(2,1)} %param.10), channel_id=1, source_target_pairs={{0,13},{1,14},{2,15},{3,0},{4,1},{5,2},{6,3},{7,4},{8,5},{9,6},{10... | collective-permute-start | bytes 983048 | tf_op jit(solution)/shard_map/ppermute | solution.py:15
  5.6 1.8 %constant_dynamic-update-slice_fusion.4 = bf16[20,2,64,320]{3,2,1,0:T(8,128)(2,1)} fusion(bf16[4,2,64,320]{3,2,1,0:T(8,128)(2,1)} %param.10), kind=kLoop, calls=%fused_computation.64 | loop fusion | bytes 720896
  7.4 1.3 fusion.39
  10.0 0.7 convert_element_type.69
  11.3 0.8 select_reduce_fusion.1
  12.1 0.4 collective-permute-done
  12.5 1.8 %constant_dynamic-update-slice_fusion.3 = bf16[20,2,64,320]{3,2,1,0:T(8,128)(2,1)} fusion(bf16[20,2,64,320]{3,2,1,0:T(8,128)(2,1)} %constant_dynamic-update-slice_fusion.4, bf16[4,2,64,320]{3,2,1,0:T(8,128)(2,1)} %collective-permute-done), kind=kLoop, calls=%fused_computation.63 | loop fusion | bytes 786432
  14.3 0.8 constant_dynamic-update-slice_fusion.2
  15.1 3.1 %collective-permute-done.2 = bf16[4,2,64,320]{3,2,1,0:T(8,128)(2,1)S(1)} collective-permute-done((bf16[4,2,64,320]{3,2,1,0:T(8,128)(2,1)}, bf16[4,2,64,320]{3,2,1,0:T(8,128)(2,1)S(1)}, u32[]{:S(2)}, u32[]{:S(2)}) %collective-permute-start.2) | collective-permute-done | bytes 327712 | tf_op jit(solution)/shard_map/ppermute | solution.py:15
  18.2 0.8 constant_dynamic-update-slice_fusion.1
  19.0 0.8 constant_dynamic-update-slice_fusion
  19.8 2.1 %convert_reduce_fusion = f32[20,2,64]{2,1,0:T(2,128)S(1)} fusion(bf16[20,2,64,320]{3,2,1,0:T(8,128)(2,1)} %constant_dynamic-update-slice_fusion), kind=kLoop, calls=%fused_computation.17 | loop fusion | flops 1635840 | bytes 1648640 | tf_op jit(solution)/shard_map/reduce_sum | solution.py:21
  21.9 1.1 multiply_reduce_fusion.1
  23.3 2.8 %fusion.4 = bf16[2560,320]{1,0:T(8,128)(2,1)S(1)} fusion(bf16[20,2,64,320]{3,2,1,0:T(8,128)(2,1)} %constant_dynamic-update-slice_fusion, f32[320]{0:T(512)S(1)} %copy-done.10, f32[2560]{0:T(1024)S(1)} %rsqrt.28, f32[2560]{0:T(1024)S(1)} %div.50), kind=kLoop, calls=%fused_computation.9 | loop fusion | flops 4096000 | bytes 3298560 | tf_op jit(solution)/shard_map/convert_element_type | solution.py:24
  26.1 4.5 %convolution_convert_fusion = bf16[2560,960]{0,1:T(8,128)(2,1)} fusion(bf16[2560,320]{1,0:T(8,128)(2,1)S(1)} %fusion.4, bf16[320,960]{1,0:T(8,128)(2,1)S(1)} %copy-done.12), kind=kOutput, calls=%fused_computation.1 | convolution fusion | flops 1575321600 | bytes 7168000 | tf_op jit(solution)/shard_map/dot_general | solution.py:25
  30.6 7.9 %copy.36 = bf16[2560,960]{1,0:T(8,128)(2,1)} copy(bf16[2560,960]{0,1:T(8,128)(2,1)} %convolution_convert_fusion) | data formatting | bytes 9830400 | tf_op jit(solution)/shard_map/convert_element_type | solution.py:25
  38.5 5.7 %constant_dynamic-slice_fusion.2 = (bf16[16,128,320]{2,1,0:T(8,128)(2,1)}, bf16[16,128,320]{2,1,0:T(8,128)(2,1)}, bf16[16,128,320]{2,1,0:T(8,128)(2,1)}) fusion(bf16[20,128,960]{2,1,0:T(8,128)(2,1)} %bitcast.58, s32[]{:T(128)S(6)} %select_n.28, s32[]{:T(128)S(6)} %add.114, s32[]{:T(128)S(6)} %add.113), kind=kLoop, calls=%fused_computation.84 | loop fusion | bytes 7864332 | tf_op jit(solution)/shard_map/slice | solution.py:35
  44.1 1.9 %copy.38 = bf16[16,128,320]{1,2,0:T(8,128)(2,1)S(1)} copy(bf16[16,128,320]{2,1,0:T(8,128)(2,1)} %get-tuple-element.8) | data formatting | bytes 2621440 | tf_op jit(solution)/shard_map/slice | solution.py:34
  46.0 5.1 %copy.40 = bf16[16,128,5,64]{3,0,2,1:T(8,128)(2,1)} copy(bf16[16,128,5,64]{1,3,2,0:T(8,128)(2,1)S(1)} %bitcast.61) | data formatting | bytes 2621440 | tf_op jit(solution)/shard_map/reshape | solution.py:34
  51.1 1.9 %copy.39 = bf16[16,128,320]{1,2,0:T(8,128)(2,1)S(1)} copy(bf16[16,128,320]{2,1,0:T(8,128)(2,1)} %get-tuple-element.7) | data formatting | bytes 2621440 | tf_op jit(solution)/shard_map/slice | solution.py:35
  53.0 5.1 %copy.41 = bf16[16,128,5,64]{3,0,2,1:T(8,128)(2,1)} copy(bf16[16,128,5,64]{1,3,2,0:T(8,128)(2,1)S(1)} %bitcast.62) | data formatting | bytes 2621440 | tf_op jit(solution)/shard_map/reshape | solution.py:35
  58.1 1.9 %copy.37 = bf16[16,128,320]{1,2,0:T(8,128)(2,1)S(1)} copy(bf16[16,128,320]{2,1,0:T(8,128)(2,1)} %get-tuple-element.9) | data formatting | bytes 2621440 | tf_op jit(solution)/shard_map/slice | solution.py:36
  60.0 5.1 %copy.42 = bf16[16,128,5,64]{3,0,2,1:T(8,128)(2,1)} copy(bf16[16,128,5,64]{1,3,2,0:T(8,128)(2,1)S(1)} %bitcast.63) | data formatting | bytes 2621440 | tf_op jit(solution)/shard_map/reshape | solution.py:36
  65.2 7.4 %fusion.48 = (f32[128,5,16]{2,1,0:T(8,128)S(1)}, f32[128,5,16,16]{2,3,1,0:T(8,128)}) fusion(bf16[16,128,5,64]{3,0,2,1:T(8,128)(2,1)} %copy.40, bf16[16,128,5,64]{3,0,2,1:T(8,128)(2,1)} %copy.41), kind=kOutput, calls=%fused_computation.95 | convolution fusion | flops 21463056 | bytes 3317760 | tf_op jit(solution)/shard_map/sub | solution.py:41
  72.5 6.7 %fusion.11 = f32[16,128,5,64]{3,0,2,1:T(8,128)} fusion(bf16[16,128,5,64]{3,0,2,1:T(8,128)(2,1)} %copy.42, f32[128,5,16,16]{2,3,1,0:T(8,128)} %get-tuple-element.18, f32[128,5,16]{2,1,0:T(8,128)S(1)} %get-tuple-element.17), kind=kOutput, calls=%fused_computation.16 | convolution fusion | flops 21299200 | bytes 4628480 | tf_op jit(solution)/shard_map/phjk,kphd->jphd/dot_general | solution.py:43
  79.2 6.2 %copy.44 = f32[16,128,5,64]{1,3,2,0:T(8,128)} copy(f32[16,128,5,64]{3,0,2,1:T(8,128)} %fusion.11) | data formatting | bytes 5242880 | tf_op jit(solution)/shard_map/phjk,kphd->jphd/transpose | solution.py:43
  85.4 2.1 %fusion.8 = bf16[16,128,320]{1,2,0:T(8,128)(2,1)S(1)} fusion(f32[16,128,5,64]{1,3,2,0:T(8,128)} %copy.44, f32[16]{0:T(128)S(1)} %convert_element_type.69), kind=kLoop, calls=%fused_computation.13 | loop fusion | flops 1310720 | bytes 3932224 | tf_op jit(solution)/shard_map/convert_element_type | solution.py:46
  87.5 1.6 %copy.45 = bf16[16,128,320]{2,1,0:T(8,128)(2,1)} copy(bf16[16,128,320]{1,2,0:T(8,128)(2,1)S(1)} %fusion.8) | data formatting | bytes 2621440 | tf_op jit(solution)/shard_map/convert_element_type | solution.py:46
  89.1 0.3 broadcast_in_dim.26
  89.3 1.1 copy-done.5
  90.5 0.3 constant_dynamic-update-slice_fusion.5
  90.8 1.1 fusion.46
  91.9 1.9 %copy.62 = bf16[4,128,320]{1,2,0:T(8,128)(2,1)} copy(bf16[4,128,320]{2,1,0:T(8,128)(2,1)} %get-tuple-element.12) | data formatting | bytes 655360
  93.8 16.5 %collective-permute-start.4 = (bf16[4,128,320]{1,2,0:T(8,128)(2,1)}, bf16[4,128,320]{1,2,0:T(8,128)(2,1)}, u32[]{:S(2)}, u32[]{:S(2)}) collective-permute-start(bf16[4,128,320]{1,2,0:T(8,128)(2,1)} %copy.62), channel_id=1, source_target_pairs={{0,1},{1,2},{2,3},{3,4},{4,5},{5,6},{6,7},{7,8},{8,9},{9,10},{10,1... | collective-permute-start | bytes 983048 | tf_op jit(solution)/shard_map/ppermute | solution.py:15
  110.3 0.9 copy.63
  111.2 0.9 copy.64
  112.1 1.6 %collective-permute-start.6 = (bf16[4,128,320]{1,2,0:T(8,128)(2,1)}, bf16[4,128,320]{1,2,0:T(8,128)(2,1)}, u32[]{:S(2)}, u32[]{:S(2)}) collective-permute-start(bf16[4,128,320]{1,2,0:T(8,128)(2,1)} %copy.64), channel_id=1, source_target_pairs={{0,3},{1,4},{2,5},{3,6},{4,7},{5,8},{6,9},{7,10},{8,11},{9,12},{10... | collective-permute-start | bytes 983048 | tf_op jit(solution)/shard_map/ppermute | solution.py:15
  113.8 0.2 select_reduce_fusion
  114.0 3.1 %collective-permute-start.7 = (bf16[4,128,320]{2,1,0:T(8,128)(2,1)}, bf16[4,128,320]{2,1,0:T(8,128)(2,1)}, u32[]{:S(2)}, u32[]{:S(2)}) collective-permute-start(bf16[4,128,320]{2,1,0:T(8,128)(2,1)} %get-tuple-element.10), channel_id=1, source_target_pairs={{0,4},{1,5},{2,6},{3,7},{4,8},{5,9},{6,10},{7,11},{8,12},{9,13},{1... | collective-permute-start | bytes 983048 | tf_op jit(solution)/shard_map/ppermute | solution.py:15
  117.1 0.2 copy.61
  117.3 6.3 %collective-permute-done.5 = bf16[4,128,320]{1,2,0:T(8,128)(2,1)} collective-permute-done((bf16[4,128,320]{1,2,0:T(8,128)(2,1)}, bf16[4,128,320]{1,2,0:T(8,128)(2,1)}, u32[]{:S(2)}, u32[]{:S(2)}) %collective-permute-start.5) | collective-permute-done | bytes 327712 | tf_op jit(solution)/shard_map/ppermute | solution.py:15
  123.7 7.0 %collective-permute-done.6 = bf16[4,128,320]{1,2,0:T(8,128)(2,1)} collective-permute-done((bf16[4,128,320]{1,2,0:T(8,128)(2,1)}, bf16[4,128,320]{1,2,0:T(8,128)(2,1)}, u32[]{:S(2)}, u32[]{:S(2)}) %collective-permute-start.6) | collective-permute-done | bytes 327712 | tf_op jit(solution)/shard_map/ppermute | solution.py:15
  130.7 2.2 %convert_add_fusion = f32[4,128,320]{1,2,0:T(8,128)} fusion(bf16[4,128,320]{1,2,0:T(8,128)(2,1)} %collective-permute-done.6, bf16[4,128,320]{1,2,0:T(8,128)(2,1)} %collective-permute-done.5, bf16[4,128,320]{1,2,0:T(8,128)(2,1)} %collective-permute-done.4, bf16[4,128,320]{1,2,0:T(8,128)(2,1)S(1)} %copy.61), kind=kLoop, calls=%fused_computation.41 | loop fusion | flops 1146880 | bytes 1966080 | tf_op jit(solution)/shard_map/add | solution.py:93
  132.9 1.3 copy.50
  134.2 6.5 %collective-permute-done.7 = bf16[4,128,320]{2,1,0:T(8,128)(2,1)} collective-permute-done((bf16[4,128,320]{2,1,0:T(8,128)(2,1)}, bf16[4,128,320]{2,1,0:T(8,128)(2,1)}, u32[]{:S(2)}, u32[]{:S(2)}) %collective-permute-start.7) | collective-permute-done | bytes 327712 | tf_op jit(solution)/shard_map/ppermute | solution.py:15
  140.7 1.1 divide_convert_fusion.4
  141.9 1.3 fusion.49
  144.2 0.2 fusion.35
  144.5 0.3 copy.66
  145.0 0.3 fusion.27
  145.3 1.9 %fusion.12 = f32[2,32,9,320]{3,1,2,0:T(8,128)S(1)} fusion(bf16[3,3,320,320]{3,2,1,0:T(8,128)(2,1)S(1)} %copy-done, bf16[2,4,8,11,320]{4,1,3,2,0:T(4,128)(2,1)S(1)} %fusion.27, f32[320]{0:T(512)S(1)} %copy-done.7, pred[32,9]{0,1:T(8,128)(4,1)S(1)} %copy-done.8), kind=kOutput, calls=%fused_computation.19 | convolution fusion | flops 708157440 | bytes 3032608 | tf_op jit(solution)/shard_map/conv_general_dilated | solution.py:60
  147.3 0.7 copy.53
  148.0 0.2 slice_reduce_fusion.1
  148.6 0.2 broadcast.163
  148.8 0.9 copy-done.4
  149.9 0.7 copy.55
  150.6 0.2 slice_reduce_fusion
  151.2 0.2 broadcast.164
  151.4 1.6 %select_bitcast_fusion = bf16[2,4,8,9,320]{4,2,1,3,0:T(8,128)(2,1)S(1)} fusion(pred[32,9]{0,1:T(8,128)(4,1)S(1)} %copy-done.8, f32[320]{0:T(512)S(1)} %get-tuple-element.6, f32[2,32,9,320]{3,0,2,1:T(2,128)S(1)} %bitcast.64, f32[2,32,9,320]{3,1,2,0:T(8,128)S(1)} %fusion.12, f32[2,32,9,320]{3,0,2,1:T(2,128)} %bitcast.60), kind=kLoop, calls=%fused_computation.54 | loop fusion | flops 1658880 | bytes 2582048 | tf_op jit(solution)/shard_map/convert_element_type | solution.py:56
  153.1 1.9 %fusion.23 = f32[2,32,9,320]{3,1,2,0:T(8,128)S(1)} fusion(bf16[3,3,320,320]{3,2,1,0:T(8,128)(2,1)S(1)} %copy-done.11, bf16[2,4,7,1,320]{4,2,1,3,0:T(8,128)(2,1)S(1)} %get-tuple-element.16, bf16[2,4,7,1,320]{4,2,1,3,0:T(8,128)(2,1)S(1)} %get-tuple-element.15, bf16[2,4,8,9,320]{4,2,1,3,0:T(8,128)(2,1)S(1)} %select_bitcast_fusion), kind=kOutput, calls=%fused_computation.44 | convolution fusion | flops 710041600 | bytes 3020800 | tf_op jit(solution)/shard_map/conv_general_dilated | solution.py:60
  155.0 0.7 copy.57
  155.7 0.3 slice.56
  156.2 0.8 fusion.20
  (63 shorter events, 2.8 us)
Async XLA Ops:
  0.0 145.3 %copy-start = (bf16[3,3,320,320]{3,2,1,0:T(8,128)(2,1)S(1)}, bf16[3,3,320,320]{3,2,1,0:T(8,128)(2,1)}, u32[]{:S(2)}) copy-start(bf16[3,3,320,320]{3,2,1,0:T(8,128)(2,1)} %param.15) | copy-start | bytes 5529604
  0.0 12.5 %collective-permute-start = (bf16[4,2,64,320]{3,2,1,0:T(8,128)(2,1)}, bf16[4,2,64,320]{3,2,1,0:T(8,128)(2,1)}, u32[]{:S(2)}, u32[]{:S(2)}) collective-permute-start(bf16[4,2,64,320]{3,2,1,0:T(8,128)(2,1)} %param.10), channel_id=1, source_target_pairs={{0,15},{1,0},{2,1},{3,2},{4,3},{5,4},{6,5},{7,6},{8,7},{9,8},{10,9... | collective-permute-start | bytes 983048 | tf_op jit(solution)/shard_map/ppermute | solution.py:15
  0.7 13.6 %collective-permute-start.1 = (bf16[4,2,64,320]{3,2,1,0:T(8,128)(2,1)}, bf16[4,2,64,320]{3,2,1,0:T(8,128)(2,1)S(1)}, u32[]{:S(2)}, u32[]{:S(2)}) collective-permute-start(bf16[4,2,64,320]{3,2,1,0:T(8,128)(2,1)} %param.10), channel_id=1, source_target_pairs={{0,14},{1,15},{2,0},{3,1},{4,2},{5,3},{6,4},{7,5},{8,6},{9,7},{10,... | collective-permute-start | bytes 983048 | tf_op jit(solution)/shard_map/ppermute | solution.py:15
  0.7 17.5 %collective-permute-start.2 = (bf16[4,2,64,320]{3,2,1,0:T(8,128)(2,1)}, bf16[4,2,64,320]{3,2,1,0:T(8,128)(2,1)S(1)}, u32[]{:S(2)}, u32[]{:S(2)}) collective-permute-start(bf16[4,2,64,320]{3,2,1,0:T(8,128)(2,1)} %param.10), channel_id=1, source_target_pairs={{0,13},{1,14},{2,15},{3,0},{4,1},{5,2},{6,3},{7,4},{8,5},{9,6},{10... | collective-permute-start | bytes 983048 | tf_op jit(solution)/shard_map/ppermute | solution.py:15
  5.4 13.6 %collective-permute-start.3 = (bf16[4,2,64,320]{3,2,1,0:T(8,128)(2,1)}, bf16[4,2,64,320]{3,2,1,0:T(8,128)(2,1)S(1)}, u32[]{:S(2)}, u32[]{:S(2)}) collective-permute-start(bf16[4,2,64,320]{3,2,1,0:T(8,128)(2,1)} %param.10), channel_id=1, source_target_pairs={{0,12},{1,13},{2,14},{3,15},{4,0},{5,1},{6,2},{7,3},{8,4},{9,5},{1... | collective-permute-start | bytes 983048 | tf_op jit(solution)/shard_map/ppermute | solution.py:15
  19.8 2.1 %copy-start.1 = (bf16[20,2,64,320]{3,2,1,0:T(8,128)(2,1)S(1)}, bf16[20,2,64,320]{3,2,1,0:T(8,128)(2,1)}, u32[]{:S(2)}) copy-start(bf16[20,2,64,320]{3,2,1,0:T(8,128)(2,1)} %constant_dynamic-update-slice_fusion) | copy-start | bytes 4915204
  19.8 3.5 %copy-start.10 = (f32[320]{0:T(512)S(1)}, f32[320]{0:T(512)}, u32[]{:S(2)}) copy-start(f32[320]{0:T(512)} %param.11) | copy-start | bytes 3844
  23.1 3.0 %copy-start.12 = (bf16[320,960]{1,0:T(8,128)(2,1)S(1)}, bf16[320,960]{1,0:T(8,128)(2,1)}, u32[]{:S(2)}) copy-start(bf16[320,960]{1,0:T(8,128)(2,1)} %param.12) | copy-start | bytes 1843204
  89.1 1.4 copy-start.5
  90.8 26.3 %copy-start.9 = (f32[2,320]{1,0:T(2,128)S(1)}, f32[2,320]{1,0:T(2,128)}, u32[]{:S(2)}) copy-start(f32[2,320]{1,0:T(2,128)} %param.14) | copy-start | bytes 7684
  93.8 23.5 %collective-permute-start.4 = (bf16[4,128,320]{1,2,0:T(8,128)(2,1)}, bf16[4,128,320]{1,2,0:T(8,128)(2,1)}, u32[]{:S(2)}, u32[]{:S(2)}) collective-permute-start(bf16[4,128,320]{1,2,0:T(8,128)(2,1)} %copy.62), channel_id=1, source_target_pairs={{0,1},{1,2},{2,3},{3,4},{4,5},{5,6},{6,7},{7,8},{8,9},{9,10},{10,1... | collective-permute-start | bytes 983048 | tf_op jit(solution)/shard_map/ppermute | solution.py:15
  111.2 12.5 %collective-permute-start.5 = (bf16[4,128,320]{1,2,0:T(8,128)(2,1)}, bf16[4,128,320]{1,2,0:T(8,128)(2,1)}, u32[]{:S(2)}, u32[]{:S(2)}) collective-permute-start(bf16[4,128,320]{1,2,0:T(8,128)(2,1)} %copy.63), channel_id=1, source_target_pairs={{0,2},{1,3},{2,4},{3,5},{4,6},{5,7},{6,8},{7,9},{8,10},{9,11},{10,... | collective-permute-start | bytes 983048 | tf_op jit(solution)/shard_map/ppermute | solution.py:15
  112.1 18.6 %collective-permute-start.6 = (bf16[4,128,320]{1,2,0:T(8,128)(2,1)}, bf16[4,128,320]{1,2,0:T(8,128)(2,1)}, u32[]{:S(2)}, u32[]{:S(2)}) collective-permute-start(bf16[4,128,320]{1,2,0:T(8,128)(2,1)} %copy.64), channel_id=1, source_target_pairs={{0,3},{1,4},{2,5},{3,6},{4,7},{5,8},{6,9},{7,10},{8,11},{9,12},{10... | collective-permute-start | bytes 983048 | tf_op jit(solution)/shard_map/ppermute | solution.py:15
  114.0 26.8 %collective-permute-start.7 = (bf16[4,128,320]{2,1,0:T(8,128)(2,1)}, bf16[4,128,320]{2,1,0:T(8,128)(2,1)}, u32[]{:S(2)}, u32[]{:S(2)}) collective-permute-start(bf16[4,128,320]{2,1,0:T(8,128)(2,1)} %get-tuple-element.10), channel_id=1, source_target_pairs={{0,4},{1,5},{2,6},{3,7},{4,8},{5,9},{6,10},{7,11},{8,12},{9,13},{1... | collective-permute-start | bytes 983048 | tf_op jit(solution)/shard_map/ppermute | solution.py:15
  117.3 24.6 %copy-start.6 = (bf16[4,2,64,320]{3,2,1,0:T(8,128)(2,1)S(1)}, bf16[4,2,64,320]{3,2,1,0:T(8,128)(2,1)}, u32[]{:S(2)}) copy-start(bf16[4,2,64,320]{3,2,1,0:T(8,128)(2,1)} %param.10) | copy-start | bytes 983044
  143.2 1.8 %copy-start.2 = (f32[4,2,64,320]{3,2,1,0:T(8,128)}, f32[4,2,64,320]{3,2,1,0:T(8,128)S(1)}, u32[]{:S(2)}) copy-start(f32[4,2,64,320]{3,2,1,0:T(8,128)S(1)} %get-tuple-element.20) | copy-start | bytes 1966084
  143.8 1.5 copy-start.7
  143.8 1.5 copy-start.8
  148.8 0.9 copy-start.4
  151.2 1.9 %copy-start.11 = (bf16[3,3,320,320]{3,2,1,0:T(8,128)(2,1)S(1)}, bf16[3,3,320,320]{3,2,1,0:T(8,128)(2,1)}, u32[]{:S(2)}) copy-start(bf16[3,3,320,320]{3,2,1,0:T(8,128)(2,1)} %param.16) | copy-start | bytes 5529604
  155.0 1.1 copy-start.3
where the time goes:
time: 158 us; the launch traced here: 157 us
  local copies, waits for them, and re-layouts  62.2 us (39%)
  starting transfers between devices  26.8 us (17%)
  matrix products  23.8 us (15%)
  waiting for transfers between devices  23.4 us (15%)
  other arithmetic  18.4 us (12%)
  between operations  2.43 us (2%)
    ppermute x8, starting transfers between devices, shifted(): lax.ppermute(shard, axis, [(i, (i + by) % count) for i in range(count)])  26.8 us
    ppermute x8, waiting for transfers between devices, shifted(): lax.ppermute(shard, axis, [(i, (i + by) % count) for i in range(count)])  23.4 us
    unnamed x35, local copies, waits for them, and re-layouts  11.7 us
    convert_element_type x1, local copies, waits for them, and re-layouts, layer_project(): jnp.dot(normed.reshape(-1, channels), w_qkv, preferred_element_type=jnp.f...  7.87 us
    slice x2, local copies, waits for them, and re-layouts, window_attend(): window[..., channels:2 * channels]  7.52 us
    sub x1, matrix products, window_attend(): expos = jnp.exp(scores - highest)  7.4 us
    dot_general x1, matrix products, window_attend(): jnp.einsum('phjk,kphd->jphd', probs, values, preferred_element_type=jnp.f...  6.67 us
    transpose x1, local copies, waits for them, and re-layouts, window_attend(): jnp.einsum('phjk,kphd->jphd', probs, values, preferred_element_type=jnp.f...  6.18 us
  transfers between devices with their start and end apart: 8, of which 5 were waited for; matrix products, arithmetic and copies ran while one was open for 9% of the time, Pallas kernels for 0%

commit v1 on v0

v1 whole, which is shorter than its diff:
```python
import functools

import jax
import jax.numpy as jnp
from jax import lax
from jax.experimental import pallas as pl
from jax.experimental.pallas import tpu as pltpu
from jax.sharding import PartitionSpec as P

HEADS = 5
HEAD_DIM = 64
NORM_GROUPS = 32
WINDOW = 16
LANES = 128
EPS = 1e-05
FAR = -1e30
F32 = jnp.float32
BF16 = jnp.bfloat16
MESH = pl.DeviceIdType.MESH
VMEM = pl.BlockSpec(memory_space=pltpu.VMEM)
SMEM = pl.BlockSpec(memory_space=pltpu.SMEM)
ANY = pl.BlockSpec(memory_space=pl.ANY)


def meet(count):
    me = lax.axis_index("frame")
    barrier = pltpu.get_barrier_semaphore()
    for step in range(1, count):
        pl.semaphore_signal(
            barrier, inc=1, device_id={"frame": lax.rem(me + step, count)}, device_id_type=MESH
        )
    pl.semaphore_wait(barrier, count - 1)


def exchange(count, source, target, send_sem, recv_sem, own_sem):
    me = lax.axis_index("frame")
    copies = []
    for step in range(1, count):
        peer = lax.rem(me + step, count)
        copy = pltpu.make_async_remote_copy(
            src_ref=source(peer),
            dst_ref=target(me),
            send_sem=send_sem.at[step],
            recv_sem=recv_sem.at[step],
            device_id={"frame": peer},
            device_id_type=MESH,
        )
        copy.start()
        copies.append(copy)
    own = pltpu.make_async_copy(source(me), target(me), own_sem)
    own.start()
    own.wait()
    for copy in copies:
        copy.wait()


def spread_kernel(count, x_ref, y_ref, send_sem, recv_sem, own_sem):
    meet(count)
    exchange(count, lambda i: x_ref.at[:, i], lambda i: y_ref.at[i], send_sem, recv_sem, own_sem)


def gather_kernel(count, y_ref, z_ref, send_sem, recv_sem, own_sem):
    meet(count)
    exchange(count, lambda i: y_ref.at[i], lambda i: z_ref.at[:, i], send_sem, recv_sem, own_sem)


def transfer(kernel, count, array, shape, identity):
    return pl.pallas_call(
        functools.partial(kernel, count),
        out_shape=jax.ShapeDtypeStruct(shape, array.dtype),
        in_specs=[ANY],
        out_specs=ANY,
        scratch_shapes=[
            pltpu.SemaphoreType.DMA((count,)),
            pltpu.SemaphoreType.DMA((count,)),
            pltpu.SemaphoreType.DMA,
        ],
        compiler_params=pltpu.CompilerParams(collective_id=identity, has_side_effects=True),
    )(array)


def mod_lane(shape, width, copies):
    lane = lax.broadcasted_iota(jnp.int32, shape, 1)
    out = lane
    for at in range(1, copies):
        out = jnp.where(lane >= at * width, lane - at * width, out)
    return out


def window_tables(frames, block, nblocks, copies, offsets_ref, numer_ref):
    reach = WINDOW // block
    width = copies * frames
    frame = mod_lane((1, width), frames, copies)
    rows = []
    for back in range(reach + 1):
        start = jnp.zeros((1, width), jnp.int32)
        for w in range(nblocks):
            first = block * ((w + back) % nblocks)
            start = jnp.where(
                (frame >= first) & (frame < first + block), block * w + offsets_ref[w], start
            )
        spot = frame - start
        spot = jnp.where(spot < 0, spot + frames, spot)
        spot = jnp.where(spot < 0, spot + frames, spot)
        numer = jnp.zeros((1, width), F32)
        for j in range(WINDOW):
            numer = jnp.where(spot == j, numer_ref[j].astype(F32), numer)
        rows.append((start, numer))
    total = rows[0][1]
    for _, numer in rows[1:]:
        total = total + numer
    key = lax.broadcasted_iota(jnp.int32, (frames, width), 0)
    tables = []
    for start, numer in rows:
        spot = key - start
        spot = jnp.where(spot < 0, spot + frames, spot)
        spot = jnp.where(spot < 0, spot + frames, spot)
        tables.append((jnp.where(spot < WINDOW, 0.0, FAR).astype(F32), numer / total))
    return tables


def attend(
    frames, cells, block, x_ref, gain_ref, w_ref, offsets_ref, numer_ref, out_ref,
    q_ref, k_ref, v_ref, comb_ref, bias_ref,
):
    channels = x_ref.shape[-1]
    rows = frames * cells
    nblocks = offsets_ref.shape[0]
    reach = WINDOW // block
    x = x_ref[...].astype(F32)
    average = jnp.mean(x, axis=-1, keepdims=True)
    centered = x - average
    variance = jnp.mean(centered * centered, axis=-1, keepdims=True)
    normed = (centered * lax.rsqrt(variance + EPS) * gain_ref[...]).astype(BF16)
    col = lax.broadcasted_iota(jnp.int32, (frames, rows), 1)
    row = lax.broadcasted_iota(jnp.int32, (frames, rows), 0)
    pick = jnp.concatenate(
        [jnp.where(col == row * cells + p, 1.0, 0.0).astype(BF16) for p in range(cells)], 0
    )
    normed = jnp.dot(pick, normed, preferred_element_type=F32).astype(BF16)
    for at, ref in enumerate((q_ref, k_ref, v_ref)):
        weight = w_ref[:, at * channels : (at + 1) * channels]
        ref[...] = jnp.dot(normed, weight, preferred_element_type=F32).astype(BF16)
    per = max(1, LANES // HEAD_DIM)
    tables = {}
    for first in range(0, HEADS, per):
        copies = min(per, HEADS - first)
        if copies not in tables:
            tables[copies] = None
    full = window_tables(frames, block, nblocks, per, offsets_ref, numer_ref)
    for back in range(reach + 1):
        bias_ref[back] = full[back][0]
    weights = [numer for _, numer in full]
    scale = HEAD_DIM**-0.5
    for p in range(cells):
        here = pl.ds(p * frames, frames)
        for first in range(0, HEADS, per):
            copies = min(per, HEADS - first)
            lanes = pl.ds(first * HEAD_DIM, copies * HEAD_DIM)
            q = q_ref[here, lanes]
            k = k_ref[here, lanes]
            v = v_ref[here, lanes]
            lane = lax.broadcasted_iota(jnp.int32, (frames, copies * HEAD_DIM), 1)
            spread = [
                jnp.where(
                    (lane >= h * HEAD_DIM) & (lane < (h + 1) * HEAD_DIM), q.astype(F32), 0.0
                ).astype(BF16)
                for h in range(copies)
            ]
            spread = jnp.concatenate(spread, 0) if copies > 1 else q
            scores = (
                lax.dot_general(
                    k, spread, (((1,), (1,)), ((), ())), preferred_element_type=F32
                )
                * scale
            )
            width = copies * frames
            total = jnp.zeros((frames, width), F32)
            for back in range(reach + 1):
                masked = scores + bias_ref[back, :, :width]
                expo = jnp.exp(masked - jnp.max(masked, axis=0, keepdims=True))
                level = weights[back][:, :width] / jnp.sum(expo, axis=0, keepdims=True)
                total = total + expo * level
            mixed = lax.dot_general(
                total.T.astype(BF16), v, (((1,), (0,)), ((), ())), preferred_element_type=F32
            )
            out = mixed[:frames]
            for h in range(1, copies):
                out = jnp.where(lane >= h * HEAD_DIM, mixed[h * frames : (h + 1) * frames], out)
            comb_ref[here, lanes] = out.astype(BF16)
    tall = lax.broadcasted_iota(jnp.int32, (rows, frames), 0)
    wide = lax.broadcasted_iota(jnp.int32, (rows, frames), 1)
    result = jnp.zeros((rows, channels), F32)
    for p in range(cells):
        back_pick = jnp.where(tall == wide * cells + p, 1.0, 0.0).astype(BF16)
        result = result + jnp.dot(
            back_pick, comb_ref[pl.ds(p * frames, frames), :], preferred_element_type=F32
        )
    out_ref[...] = result.astype(BF16)


def attention(x, gain, w_qkv, offsets, numerators, frames, cells, block):
    rows, channels = x.shape
    per = max(1, LANES // HEAD_DIM)
    return pl.pallas_call(
        functools.partial(attend, frames, cells, block),
        out_shape=jax.ShapeDtypeStruct(x.shape, BF16),
        in_specs=[VMEM, VMEM, VMEM, SMEM, SMEM],
        out_specs=VMEM,
        scratch_shapes=[pltpu.VMEM((rows, channels), BF16)] * 4
        + [pltpu.VMEM((WINDOW // block + 1, frames, per * frames), F32)],
        compiler_params=pltpu.CompilerParams(vmem_limit_bytes=60 * 2**20),
    )(x, gain, w_qkv, offsets, numerators)


def group_sum(sums):
    channels = sums.shape[-1]
    size = channels // NORM_GROUPS
    row = lax.broadcasted_iota(jnp.int32, (channels, channels), 0)
    col = lax.broadcasted_iota(jnp.int32, (channels, channels), 1)
    row_group = (row.astype(F32) * (1.0 / size) + 0.5 / size).astype(jnp.int32)
    col_group = (col.astype(F32) * (1.0 / size) + 0.5 / size).astype(jnp.int32)
    same = jnp.where(row_group == col_group, 1.0, 0.0).astype(F32)
    return jnp.dot(sums, same, preferred_element_type=F32, precision=lax.Precision.HIGHEST)


def group_act(tensor, gain):
    cells, channels = tensor[0].shape
    count = cells * (channels // NORM_GROUPS)
    sums = jnp.concatenate([jnp.sum(t, axis=0, keepdims=True) for t in tensor], 0)
    average = group_sum(sums) * (1.0 / count)
    centered = [t - average[i : i + 1] for i, t in enumerate(tensor)]
    squares = jnp.concatenate([jnp.sum(c * c, axis=0, keepdims=True) for c in centered], 0)
    factor = lax.rsqrt(group_sum(squares) * (1.0 / count) + EPS) * gain
    normed = [c * factor[i : i + 1] for i, c in enumerate(centered)]
    return [v / (1.0 + jnp.exp(-v)) for v in normed]


def conv_three(acts, conv_ref, tile_rows, tile_cols):
    count = len(acts)
    lines = []
    for r in range(tile_rows):
        line = jnp.concatenate([a[r * tile_cols : (r + 1) * tile_cols] for a in acts], 0)
        length = line.shape[0]
        at = jnp.concatenate(
            [lax.broadcasted_iota(jnp.int32, (tile_cols, line.shape[1]), 0)] * count, 0
        )
        before = jnp.where(at == 0, 0.0, pltpu.roll(line, 1, 0))
        after = jnp.where(at == tile_cols - 1, 0.0, pltpu.roll(line, length - 1, 0))
        lines.append([before.astype(BF16), line.astype(BF16), after.astype(BF16)])
    outs = []
    for r in range(tile_rows):
        total = None
        for s in range(max(0, r - 1), min(tile_rows, r + 2)):
            for x in range(3):
                term = jnp.dot(lines[s][x], conv_ref[s - r + 1, x], preferred_element_type=F32)
                total = term if total is None else total + term
        outs.append(total)
    return outs


def per_frame(lines, count, tile_cols):
    return [
        jnp.concatenate([line[i * tile_cols : (i + 1) * tile_cols] for line in lines], 0)
        for i in range(count)
    ]


def residual(
    block, tile_rows, tile_cols, x_ref, z_ref, w_out_ref, gn_ref, one_ref, two_ref, step_ref, out_ref
):
    cells = tile_rows * tile_cols
    projected = jnp.dot(z_ref[...], w_out_ref[...], preferred_element_type=F32)
    hidden = (x_ref[...].astype(F32) + projected).astype(BF16).astype(F32)
    hidden = [hidden[i * cells : (i + 1) * cells] for i in range(block)]
    acts = group_act(hidden, gn_ref[0:1])
    lines = conv_three(acts, one_ref, tile_rows, tile_cols)
    middle = per_frame([line + step_ref[...] for line in lines], block, tile_cols)
    acts = group_act(middle, gn_ref[1:2])
    lines = conv_three(acts, two_ref, tile_rows, tile_cols)
    moved = per_frame(lines, block, tile_cols)
    for i in range(block):
        out_ref[i * cells : (i + 1) * cells] = (hidden[i] + moved[i]).astype(BF16)


def resblock(x, z, w_out, gn_gain, conv_one, conv_two, step, block, tile_rows, tile_cols):
    return pl.pallas_call(
        functools.partial(residual, block, tile_rows, tile_cols),
        out_shape=jax.ShapeDtypeStruct(x.shape, BF16),
        in_specs=[VMEM] * 7,
        out_specs=VMEM,
        compiler_params=pltpu.CompilerParams(vmem_limit_bytes=60 * 2**20),
    )(x, z, w_out, gn_gain, conv_one, conv_two, step)


def body(
    latents, norm_gain, w_qkv, w_out, gn_gain, conv_one, conv_two, step_embed, offsets, numerators
):
    block, tile_rows, tile_cols, channels = latents.shape
    count = lax.axis_size("frame")
    cells = tile_rows * tile_cols // count
    frames = block * count
    split = latents.reshape(block, count, cells, channels)
    seen = transfer(spread_kernel, count, split, (count, block, cells, channels), 0)
    combined = attention(
        seen.reshape(frames * cells, channels),
        norm_gain.reshape(1, channels),
        w_qkv,
        offsets,
        numerators,
        frames,
        cells,
        block,
    )
    back = transfer(
        gather_kernel,
        count,
        combined.reshape(count, block, cells, channels),
        (block, count, cells, channels),
        1,
    )
    flat = (block * tile_rows * tile_cols, channels)
    result = resblock(
        latents.reshape(flat),
        back.reshape(flat),
        w_out,
        gn_gain,
        conv_one,
        conv_two,
        step_embed.reshape(1, channels),
        block,
        tile_rows,
        tile_cols,
    )
    return result.reshape(latents.shape)


def solution(mesh):
    return jax.shard_map(
        body,
        mesh=mesh,
        in_specs=(
            P(("groups", "frame"), None, None, None),
            P(),
            P(),
            P(),
            P(),
            P(),
            P(),
            P(),
            P("groups"),
            P(),
        ),
        out_specs=P(("groups", "frame"), None, None, None),
        check_vma=False,
    )
```

time: 158 us -> 49.2 us (0.31)
  the two profiles are of different devices: /device:TPU:5 before, /device:TPU:0 now
where the time goes in v1:
time: 49.2 us; the launch traced here: 48.4 us
  Pallas kernels  46.6 us (95%)
  local copies, waits for them, and re-layouts  1.81 us (4%)
    pallas_call x2, Pallas kernels, transfer(): pl.pallas_call(functools.partial(kernel, count), out_shape=jax.ShapeDtype...  27 us
    pallas_call x1, Pallas kernels, attention(): pl.pallas_call(functools.partial(attend, frames, cells, block), out_shape...  10.8 us
    pallas_call x1, Pallas kernels, resblock(): pl.pallas_call(functools.partial(residual, block, tile_rows, tile_cols),...  8.79 us
    reshape x1, local copies, waits for them, and re-layouts, body(): norm_gain.reshape(1, channels)  1.25 us

profile of v1, /device:TPU:0, one launch (start us, length us, event | category | flops | bytes accessed | tf_op | source)
XLA Modules:
  0.0 48.4 jit_solution(6081268877233908921)
XLA Ops:
  0.0 0.0 copy-start
  0.0 13.4 %shard_map.100 = bf16[16,4,8,320]{3,2,1,0:T(8,128)(2,1)} custom-call(bf16[4,16,8,320]{3,2,1,0:T(8,128)(2,1)} %bitcast.8), custom_call_target="tpu_custom_call" | custom-call | tf_op jit(solution)/shard_map/pallas_call | solution.py:68
  13.4 1.2 %reshape.27.gain_ref = f32[1,320]{1,0:T(1,128)} reshape(f32[320]{0:T(512)} %param.11) | data formatting | bytes 2560 | tf_op jit(solution)/shard_map/reshape | solution.py:307
  14.7 10.8 %shard_map.101 = bf16[512,320]{1,0:T(8,128)(2,1)} custom-call(bf16[512,320]{1,0:T(8,128)(2,1)} %bitcast.7, f32[1,320]{1,0:T(1,128)} %reshape.27.gain_ref, bf16[320,960]{1,0:T(8,128)(2,1)} %w_ref.1, s32[16]{0:T(128)} %offsets_ref.1, s32[16]{0:T(128)} %numer_ref.1), custom_call_target="tpu_custom_call" | custom-call | tf_op jit(solution)/shard_map/pallas_call | solution.py:205
  25.5 13.6 %shard_map.102 = bf16[4,16,8,320]{3,2,1,0:T(8,128)(2,1)} custom-call(bf16[16,4,8,320]{3,2,1,0:T(8,128)(2,1)} %bitcast.6), custom_call_target="tpu_custom_call" | custom-call | tf_op jit(solution)/shard_map/pallas_call | solution.py:68
  39.1 0.0 copy-done
  39.1 0.6 %reshape.30.step_ref = f32[1,320]{1,0:T(1,128)} reshape(f32[320]{0:T(512)S(1)} %copy-done) | data formatting | bytes 2560 | tf_op jit(solution)/shard_map/reshape | solution.py:330
  39.6 8.8 %shard_map.103 = bf16[512,320]{1,0:T(8,128)(2,1)} custom-call(bf16[512,320]{1,0:T(8,128)(2,1)} %bitcast.9, bf16[512,320]{1,0:T(8,128)(2,1)} %bitcast.10, bf16[320,320]{1,0:T(8,128)(2,1)} %w_out_ref.1, f32[2,320]{1,0:T(2,128)} %gn_ref.1, bf16[3,3,320,320]{3,2,1,0:T(8,128)(2,1)} %one_ref.1, bf16[3,3,320,320]{3,2,1,0:T(8,128)(2,1)} %two_ref.1, ...), custom_call_target="tpu_custom_call" | custom-call | tf_op jit(solution)/shard_map/pallas_call | solution.py:287
Async XLA Ops:
  0.0 39.1 %copy-start = (f32[320]{0:T(512)S(1)}, f32[320]{0:T(512)}, u32[]{:S(2)}) copy-start(f32[320]{0:T(512)} %param.17) | copy-start | bytes 3844

commit v2 on v1

--- a/solution.py
+++ b/solution.py
@@ -32,51 +32,15 @@
     pl.semaphore_wait(barrier, count - 1)
 
 
-def exchange(count, source, target, send_sem, recv_sem, own_sem):
-    me = lax.axis_index("frame")
-    copies = []
-    for step in range(1, count):
-        peer = lax.rem(me + step, count)
-        copy = pltpu.make_async_remote_copy(
-            src_ref=source(peer),
-            dst_ref=target(me),
-            send_sem=send_sem.at[step],
-            recv_sem=recv_sem.at[step],
-            device_id={"frame": peer},
-            device_id_type=MESH,
-        )
-        copy.start()
-        copies.append(copy)
-    own = pltpu.make_async_copy(source(me), target(me), own_sem)
-    own.start()
-    own.wait()
-    for copy in copies:
-        copy.wait()
-
-
-def spread_kernel(count, x_ref, y_ref, send_sem, recv_sem, own_sem):
-    meet(count)
-    exchange(count, lambda i: x_ref.at[:, i], lambda i: y_ref.at[i], send_sem, recv_sem, own_sem)
-
-
-def gather_kernel(count, y_ref, z_ref, send_sem, recv_sem, own_sem):
-    meet(count)
-    exchange(count, lambda i: y_ref.at[i], lambda i: z_ref.at[:, i], send_sem, recv_sem, own_sem)
-
-
-def transfer(kernel, count, array, shape, identity):
-    return pl.pallas_call(
-        functools.partial(kernel, count),
-        out_shape=jax.ShapeDtypeStruct(shape, array.dtype),
-        in_specs=[ANY],
-        out_specs=ANY,
-        scratch_shapes=[
-            pltpu.SemaphoreType.DMA((count,)),
-            pltpu.SemaphoreType.DMA((count,)),
-            pltpu.SemaphoreType.DMA,
-        ],
-        compiler_params=pltpu.CompilerParams(collective_id=identity, has_side_effects=True),
-    )(array)
+def remote(source, target, send_sem, recv_sem, peer):
+    return pltpu.make_async_remote_copy(
+        src_ref=source,
+        dst_ref=target,
+        send_sem=send_sem,
+        recv_sem=recv_sem,
+        device_id={"frame": peer},
+        device_id_type=MESH,
+    )
 
 
 def mod_lane(shape, width, copies):
@@ -120,61 +84,84 @@
 
 
 def attend(
-    frames, cells, block, x_ref, gain_ref, w_ref, offsets_ref, numer_ref, out_ref,
-    q_ref, k_ref, v_ref, comb_ref, bias_ref,
+    count, x_ref, gain_ref, w_ref, offsets_ref, numer_ref, z_ref,
+    seen_ref, q_ref, k_ref, v_ref, comb_ref, ready_ref, bias_ref, pick_ref, place_ref,
+    send_sem, recv_sem, own_sem, back_send, back_recv, back_own,
 ):
-    channels = x_ref.shape[-1]
+    block, _, cells, channels = x_ref.shape
+    frames = block * count
     rows = frames * cells
     nblocks = offsets_ref.shape[0]
     reach = WINDOW // block
-    x = x_ref[...].astype(F32)
-    average = jnp.mean(x, axis=-1, keepdims=True)
-    centered = x - average
-    variance = jnp.mean(centered * centered, axis=-1, keepdims=True)
-    normed = (centered * lax.rsqrt(variance + EPS) * gain_ref[...]).astype(BF16)
+    per = max(1, LANES // HEAD_DIM)
+    me = lax.axis_index("frame")
+    meet(count)
+    copies = []
+    for step in range(1, count):
+        peer = lax.rem(me + step, count)
+        copy = remote(
+            x_ref.at[:, peer], seen_ref.at[me], send_sem.at[step], recv_sem.at[step], peer
+        )
+        copy.start()
+        copies.append(copy)
+    own = pltpu.make_async_copy(x_ref.at[:, me], seen_ref.at[me], own_sem)
+    own.start()
+
     col = lax.broadcasted_iota(jnp.int32, (frames, rows), 1)
     row = lax.broadcasted_iota(jnp.int32, (frames, rows), 0)
-    pick = jnp.concatenate(
-        [jnp.where(col == row * cells + p, 1.0, 0.0).astype(BF16) for p in range(cells)], 0
-    )
-    normed = jnp.dot(pick, normed, preferred_element_type=F32).astype(BF16)
-    for at, ref in enumerate((q_ref, k_ref, v_ref)):
-        weight = w_ref[:, at * channels : (at + 1) * channels]
-        ref[...] = jnp.dot(normed, weight, preferred_element_type=F32).astype(BF16)
-    per = max(1, LANES // HEAD_DIM)
-    tables = {}
-    for first in range(0, HEADS, per):
-        copies = min(per, HEADS - first)
-        if copies not in tables:
-            tables[copies] = None
+    for p in range(cells):
+        pick_ref[p * frames : (p + 1) * frames] = jnp.where(
+            col == row * cells + p, 1.0, 0.0
+        ).astype(BF16)
+    lane = lax.broadcasted_iota(jnp.int32, (1, rows), 1)
+    spot = lane * cells
+    for p in range(1, cells):
+        spot = jnp.where(lane >= p * frames, (lane - p * frames) * cells + p, spot)
+    place_ref[...] = jnp.where(
+        lax.broadcasted_iota(jnp.int32, (rows, rows), 0) == spot, 1.0, 0.0
+    ).astype(BF16)
+    comb_ref[...] = jnp.zeros_like(comb_ref)
     full = window_tables(frames, block, nblocks, per, offsets_ref, numer_ref)
     for back in range(reach + 1):
         bias_ref[back] = full[back][0]
     weights = [numer for _, numer in full]
+
+    own.wait()
+    for copy in copies:
+        copy.wait()
+    x = seen_ref[...].astype(F32).reshape(rows, channels)
+    average = jnp.mean(x, axis=-1, keepdims=True)
+    centered = x - average
+    variance = jnp.mean(centered * centered, axis=-1, keepdims=True)
+    normed = (centered * lax.rsqrt(variance + EPS) * gain_ref[...][None, :]).astype(BF16)
+    normed = jnp.dot(pick_ref[...], normed, preferred_element_type=F32).astype(BF16)
+    for at, ref in enumerate((q_ref, k_ref, v_ref)):
+        weight = w_ref[:, at * channels : (at + 1) * channels]
+        ref[...] = jnp.dot(normed, weight, preferred_element_type=F32).astype(BF16)
     scale = HEAD_DIM**-0.5
-    for p in range(cells):
-        here = pl.ds(p * frames, frames)
-        for first in range(0, HEADS, per):
-            copies = min(per, HEADS - first)
-            lanes = pl.ds(first * HEAD_DIM, copies * HEAD_DIM)
+    returns = []
+    for chunk, first in enumerate(range(0, HEADS, per)):
+        heads = min(per, HEADS - first)
+        size = heads * HEAD_DIM
+        lanes = pl.ds(first * HEAD_DIM, size)
+        lane = lax.broadcasted_iota(jnp.int32, (frames, size), 1)
+        masks = [
+            jnp.where((lane >= h * HEAD_DIM) & (lane < (h + 1) * HEAD_DIM), 1.0, 0.0).astype(BF16)
+            for h in range(heads)
+        ]
+        width = heads * frames
+        for p in range(cells):
+            here = pl.ds(p * frames, frames)
             q = q_ref[here, lanes]
             k = k_ref[here, lanes]
             v = v_ref[here, lanes]
-            lane = lax.broadcasted_iota(jnp.int32, (frames, copies * HEAD_DIM), 1)
-            spread = [
-                jnp.where(
-                    (lane >= h * HEAD_DIM) & (lane < (h + 1) * HEAD_DIM), q.astype(F32), 0.0
-                ).astype(BF16)
-                for h in range(copies)
-            ]
-            spread = jnp.concatenate(spread, 0) if copies > 1 else q
+            spread = jnp.concatenate([q * m for m in masks], 0) if heads > 1 else q
             scores = (
                 lax.dot_general(
                     k, spread, (((1,), (1,)), ((), ())), preferred_element_type=F32
                 )
                 * scale
             )
-            width = copies * frames
             total = jnp.zeros((frames, width), F32)
             for back in range(reach + 1):
                 masked = scores + bias_ref[back, :, :width]
@@ -185,31 +172,65 @@
                 total.T.astype(BF16), v, (((1,), (0,)), ((), ())), preferred_element_type=F32
             )
             out = mixed[:frames]
-            for h in range(1, copies):
+            for h in range(1, heads):
                 out = jnp.where(lane >= h * HEAD_DIM, mixed[h * frames : (h + 1) * frames], out)
-            comb_ref[here, lanes] = out.astype(BF16)
-    tall = lax.broadcasted_iota(jnp.int32, (rows, frames), 0)
-    wide = lax.broadcasted_iota(jnp.int32, (rows, frames), 1)
-    result = jnp.zeros((rows, channels), F32)
-    for p in range(cells):
-        back_pick = jnp.where(tall == wide * cells + p, 1.0, 0.0).astype(BF16)
-        result = result + jnp.dot(
-            back_pick, comb_ref[pl.ds(p * frames, frames), :], preferred_element_type=F32
-        )
-    out_ref[...] = result.astype(BF16)
-
-
-def attention(x, gain, w_qkv, offsets, numerators, frames, cells, block):
-    rows, channels = x.shape
+            comb_ref[chunk, here, :size] = out.astype(BF16)
+        ready_ref[chunk] = (
+            jnp.dot(place_ref[...], comb_ref[chunk], preferred_element_type=F32)
+            .reshape(count, block, cells, comb_ref.shape[-1])
+            .astype(BF16)
+        )
+        for step in range(1, count):
+            peer = lax.rem(me + step, count)
+            copy = remote(
+                ready_ref.at[chunk, peer],
+                z_ref.at[chunk, :, me],
+                back_send.at[chunk, step],
+                back_recv.at[chunk, step],
+                peer,
+            )
+            copy.start()
+            returns.append(copy)
+        own = pltpu.make_async_copy(
+            ready_ref.at[chunk, me], z_ref.at[chunk, :, me], back_own.at[chunk]
+        )
+        own.start()
+        returns.append(own)
+    for copy in returns:
+        copy.wait()
+
+
+def attention(x, gain, w_qkv, offsets, numerators):
+    block, count, cells, channels = x.shape
+    rows = block * count * cells
     per = max(1, LANES // HEAD_DIM)
+    chunks = -(-HEADS // per)
+    wide = per * HEAD_DIM
     return pl.pallas_call(
-        functools.partial(attend, frames, cells, block),
-        out_shape=jax.ShapeDtypeStruct(x.shape, BF16),
+        functools.partial(attend, count),
+        out_shape=jax.ShapeDtypeStruct((chunks, block, count, cells, wide), BF16),
         in_specs=[VMEM, VMEM, VMEM, SMEM, SMEM],
-        out_specs=VMEM,
-        scratch_shapes=[pltpu.VMEM((rows, channels), BF16)] * 4
-        + [pltpu.VMEM((WINDOW // block + 1, frames, per * frames), F32)],
-        compiler_params=pltpu.CompilerParams(vmem_limit_bytes=60 * 2**20),
+        out_specs=ANY,
+        scratch_shapes=[
+            pltpu.VMEM((count, block, cells, channels), BF16),
+            pltpu.VMEM((rows, channels), BF16),
+            pltpu.VMEM((rows, channels), BF16),
+            pltpu.VMEM((rows, channels), BF16),
+            pltpu.VMEM((chunks, rows, wide), BF16),
+            pltpu.VMEM((chunks, count, block, cells, wide), BF16),
+            pltpu.VMEM((WINDOW // block + 1, block * count, per * block * count), F32),
+            pltpu.VMEM((rows, rows), BF16),
+            pltpu.VMEM((rows, rows), BF16),
+            pltpu.SemaphoreType.DMA((count,)),
+            pltpu.SemaphoreType.DMA((count,)),
+            pltpu.SemaphoreType.DMA,
+            pltpu.SemaphoreType.DMA((chunks, count)),
+            pltpu.SemaphoreType.DMA((chunks, count)),
+            pltpu.SemaphoreType.DMA((chunks,)),
+        ],
+        compiler_params=pltpu.CompilerParams(
+            collective_id=0, has_side_effects=True, vmem_limit_bytes=40 * 2**20
+        ),
     )(x, gain, w_qkv, offsets, numerators)
 
 
@@ -270,12 +291,19 @@
     block, tile_rows, tile_cols, x_ref, z_ref, w_out_ref, gn_ref, one_ref, two_ref, step_ref, out_ref
 ):
     cells = tile_rows * tile_cols
-    projected = jnp.dot(z_ref[...], w_out_ref[...], preferred_element_type=F32)
+    channels, wide = x_ref.shape[-1], z_ref.shape[-1]
+    projected = 0.0
+    for chunk in range(z_ref.shape[0]):
+        first = chunk * wide
+        size = min(wide, channels - first)
+        projected = projected + jnp.dot(
+            z_ref[chunk, :, :size], w_out_ref[first : first + size], preferred_element_type=F32
+        )
     hidden = (x_ref[...].astype(F32) + projected).astype(BF16).astype(F32)
     hidden = [hidden[i * cells : (i + 1) * cells] for i in range(block)]
     acts = group_act(hidden, gn_ref[0:1])
     lines = conv_three(acts, one_ref, tile_rows, tile_cols)
-    middle = per_frame([line + step_ref[...] for line in lines], block, tile_cols)
+    middle = per_frame([line + step_ref[...][None, :] for line in lines], block, tile_cols)
     acts = group_act(middle, gn_ref[1:2])
     lines = conv_three(acts, two_ref, tile_rows, tile_cols)
     moved = per_frame(lines, block, tile_cols)
@@ -299,35 +327,17 @@
     block, tile_rows, tile_cols, channels = latents.shape
     count = lax.axis_size("frame")
     cells = tile_rows * tile_cols // count
-    frames = block * count
     split = latents.reshape(block, count, cells, channels)
-    seen = transfer(spread_kernel, count, split, (count, block, cells, channels), 0)
-    combined = attention(
-        seen.reshape(frames * cells, channels),
-        norm_gain.reshape(1, channels),
-        w_qkv,
-        offsets,
-        numerators,
-        frames,
-        cells,
-        block,
-    )
-    back = transfer(
-        gather_kernel,
-        count,
-        combined.reshape(count, block, cells, channels),
-        (block, count, cells, channels),
-        1,
-    )
+    back = attention(split, norm_gain, w_qkv, offsets, numerators)
     flat = (block * tile_rows * tile_cols, channels)
     result = resblock(
         latents.reshape(flat),
-        back.reshape(flat),
+        back.reshape(back.shape[0], flat[0], back.shape[-1]),
         w_out,
         gn_gain,
         conv_one,
         conv_two,
-        step_embed.reshape(1, channels),
+        step_embed,
         block,
         tile_rows,
         tile_cols,

time: 49.2 us -> 45.3 us (0.921); the launches traced: 48.4 us -> 45 us
  Pallas kernels: 46.6 us -> 40.2 us
  local copies, waits for them, and re-layouts: 1.81 us -> 4.81 us
    pallas_call x3 -> x1, Pallas kernels: 37.8 us -> 31.4 us  [attention(): pl.pallas_call(functools.partial(attend, count), out_shape=jax.ShapeDtype...]
    unnamed x2 -> x12, local copies, waits for them, and re-layouts: 0.01 us -> 4.81 us
    reshape x2 -> x0, local copies, waits for them, and re-layouts: 1.81 us -> none  [the longest x1 1.25 us: body(): norm_gain.reshape(1, channels)]
where the time goes in v2:
time: 45.3 us; the launch traced here: 45 us
  Pallas kernels  40.2 us (89%)
  local copies, waits for them, and re-layouts  4.81 us (11%)
    pallas_call x1, Pallas kernels, attention(): pl.pallas_call(functools.partial(attend, count), out_shape=jax.ShapeDtype...  31.4 us
    pallas_call x1, Pallas kernels, resblock(): pl.pallas_call(functools.partial(residual, block, tile_rows, tile_cols),...  8.81 us
    unnamed x12, local copies, waits for them, and re-layouts  4.81 us

profile of v2, /device:TPU:0, one launch (start us, length us, event | category | flops | bytes accessed | tf_op | source)
XLA Modules:
  0.0 45.0 jit_solution(13154117906929459238)
XLA Ops:
  0.0 0.0 copy-start
  0.0 1.0 %copy-done = bf16[4,2,64,320]{3,2,1,0:T(8,128)(2,1)S(1)} copy-done((bf16[4,2,64,320]{3,2,1,0:T(8,128)(2,1)S(1)}, bf16[4,2,64,320]{3,2,1,0:T(8,128)(2,1)}, u32[]{:S(2)}) %copy-start) | copy-done | bytes 327704
  1.0 0.0 copy-start.2
  1.0 1.1 %copy-done.2 = bf16[320,960]{1,0:T(8,128)(2,1)S(1)} copy-done((bf16[320,960]{1,0:T(8,128)(2,1)S(1)}, bf16[320,960]{1,0:T(8,128)(2,1)}, u32[]{:S(2)}) %copy-start.2) | copy-done | bytes 614424
  2.1 0.0 copy-start.3
  2.1 0.7 %copy-done.3 = f32[320]{0:T(512)S(1)} copy-done((f32[320]{0:T(512)S(1)}, f32[320]{0:T(512)}, u32[]{:S(2)}) %copy-start.3) | copy-done | bytes 1304
  2.8 0.0 copy-start.4
  2.8 0.7 %copy-done.4 = s32[16]{0:T(128)S(1)} copy-done((s32[16]{0:T(128)S(1)}, s32[16]{0:T(128)}, u32[]{:S(2)}) %copy-start.4) | copy-done | bytes 88
  3.4 0.0 copy-start.5
  3.4 0.7 %copy-done.5 = s32[16]{0:T(128)S(1)} copy-done((s32[16]{0:T(128)S(1)}, s32[16]{0:T(128)}, u32[]{:S(2)}) %copy-start.5) | copy-done | bytes 88
  4.1 31.4 %shard_map.100 = bf16[3,4,16,8,128]{4,3,2,1,0:T(8,128)(2,1)S(1)} custom-call(bf16[4,16,8,320]{3,2,1,0:T(8,128)(2,1)S(1)} %bitcast.5, f32[320]{0:T(512)S(1)} %copy-done.3, bf16[320,960]{1,0:T(8,128)(2,1)S(1)} %copy-done.2, s32[16]{0:T(128)S(1)} %copy-done.4, s32[16]{0:T(128)S(1)} %copy-done.5), custom_call_target="tpu_custom_call" | custom-call | tf_op jit(solution)/shard_map/pallas_call | solution.py:209
  35.5 0.0 copy-start.1
  35.5 0.7 %copy-done.1 = bf16[3,4,16,8,128]{4,3,2,1,0:T(8,128)(2,1)} copy-done((bf16[3,4,16,8,128]{4,3,2,1,0:T(8,128)(2,1)}, bf16[3,4,16,8,128]{4,3,2,1,0:T(8,128)(2,1)S(1)}, u32[]{:S(2)}) %copy-start.1) | copy-done | bytes 393240
  36.2 8.8 %shard_map.101 = bf16[512,320]{1,0:T(8,128)(2,1)} custom-call(bf16[512,320]{1,0:T(8,128)(2,1)} %bitcast.4, bf16[3,512,128]{2,1,0:T(8,128)(2,1)} %bitcast.6, bf16[320,320]{1,0:T(8,128)(2,1)} %w_out_ref.1, f32[2,320]{1,0:T(2,128)} %gn_ref.1, bf16[3,3,320,320]{3,2,1,0:T(8,128)(2,1)} %one_ref.1, bf16[3,3,320,320]{3,2,1,0:T(8,128)(2,1)} %two_ref.1, f32[320]{0:T(512)} %step_ref.1), custom_call_target="tpu_custom_call" | custom-call | tf_op jit(solution)/shard_map/pallas_call | solution.py:315
Async XLA Ops:
  0.0 1.0 %copy-start = (bf16[4,2,64,320]{3,2,1,0:T(8,128)(2,1)S(1)}, bf16[4,2,64,320]{3,2,1,0:T(8,128)(2,1)}, u32[]{:S(2)}) copy-start(bf16[4,2,64,320]{3,2,1,0:T(8,128)(2,1)} %param.10) | copy-start | bytes 983044
  1.0 1.1 %copy-start.2 = (bf16[320,960]{1,0:T(8,128)(2,1)S(1)}, bf16[320,960]{1,0:T(8,128)(2,1)}, u32[]{:S(2)}) copy-start(bf16[320,960]{1,0:T(8,128)(2,1)} %w_ref.1) | copy-start | bytes 1843204
  2.1 0.7 %copy-start.3 = (f32[320]{0:T(512)S(1)}, f32[320]{0:T(512)}, u32[]{:S(2)}) copy-start(f32[320]{0:T(512)} %gain_ref.1) | copy-start | bytes 3844
  2.8 0.7 %copy-start.4 = (s32[16]{0:T(128)S(1)}, s32[16]{0:T(128)}, u32[]{:S(2)}) copy-start(s32[16]{0:T(128)} %offsets_ref.1) | copy-start | bytes 196
  3.4 0.7 %copy-start.5 = (s32[16]{0:T(128)S(1)}, s32[16]{0:T(128)}, u32[]{:S(2)}) copy-start(s32[16]{0:T(128)} %numer_ref.1) | copy-start | bytes 196
  35.5 0.7 %copy-start.1 = (bf16[3,4,16,8,128]{4,3,2,1,0:T(8,128)(2,1)}, bf16[3,4,16,8,128]{4,3,2,1,0:T(8,128)(2,1)S(1)}, u32[]{:S(2)}) copy-start(bf16[3,4,16,8,128]{4,3,2,1,0:T(8,128)(2,1)S(1)} %shard_map.100) | copy-start | bytes 1179652

commit v3 on v2

--- a/solution.py
+++ b/solution.py
@@ -84,8 +84,8 @@
 
 
 def attend(
-    count, x_ref, gain_ref, w_ref, offsets_ref, numer_ref, z_ref,
-    seen_ref, q_ref, k_ref, v_ref, comb_ref, ready_ref, bias_ref, pick_ref, place_ref,
+    count, x_ref, gain_ref, w_hbm, offsets_ref, numer_ref, z_ref,
+    w_ref, w_sem, seen_ref, q_ref, k_ref, v_ref, comb_ref, ready_ref, bias_ref, pick_ref, place_ref,
     send_sem, recv_sem, own_sem, back_send, back_recv, back_own,
 ):
     block, _, cells, channels = x_ref.shape
@@ -106,6 +106,8 @@
         copies.append(copy)
     own = pltpu.make_async_copy(x_ref.at[:, me], seen_ref.at[me], own_sem)
     own.start()
+    fetch = pltpu.make_async_copy(w_hbm, w_ref, w_sem)
+    fetch.start()
 
     col = lax.broadcasted_iota(jnp.int32, (frames, rows), 1)
     row = lax.broadcasted_iota(jnp.int32, (frames, rows), 0)
@@ -126,6 +128,7 @@
         bias_ref[back] = full[back][0]
     weights = [numer for _, numer in full]
 
+    fetch.wait()
     own.wait()
     for copy in copies:
         copy.wait()
@@ -209,9 +212,11 @@
     return pl.pallas_call(
         functools.partial(attend, count),
         out_shape=jax.ShapeDtypeStruct((chunks, block, count, cells, wide), BF16),
-        in_specs=[VMEM, VMEM, VMEM, SMEM, SMEM],
+        in_specs=[ANY, VMEM, ANY, SMEM, SMEM],
         out_specs=ANY,
         scratch_shapes=[
+            pltpu.VMEM(w_qkv.shape, BF16),
+            pltpu.SemaphoreType.DMA,
             pltpu.VMEM((count, block, cells, channels), BF16),
             pltpu.VMEM((rows, channels), BF16),
             pltpu.VMEM((rows, channels), BF16),
@@ -229,7 +234,7 @@
             pltpu.SemaphoreType.DMA((chunks,)),
         ],
         compiler_params=pltpu.CompilerParams(
-            collective_id=0, has_side_effects=True, vmem_limit_bytes=40 * 2**20
+            collective_id=0, has_side_effects=True, vmem_limit_bytes=62 * 2**20
         ),
     )(x, gain, w_qkv, offsets, numerators)
 
@@ -288,9 +293,14 @@
 
 
 def residual(
-    block, tile_rows, tile_cols, x_ref, z_ref, w_out_ref, gn_ref, one_ref, two_ref, step_ref, out_ref
+    block, tile_rows, tile_cols, x_ref, z_ref, w_out_ref, gn_ref, one_hbm, two_hbm, step_ref, out_ref,
+    one_ref, two_ref, one_sem, two_sem,
 ):
     cells = tile_rows * tile_cols
+    first_fetch = pltpu.make_async_copy(one_hbm, one_ref, one_sem)
+    first_fetch.start()
+    second_fetch = pltpu.make_async_copy(two_hbm, two_ref, two_sem)
+    second_fetch.start()
     channels, wide = x_ref.shape[-1], z_ref.shape[-1]
     projected = 0.0
     for chunk in range(z_ref.shape[0]):
@@ -302,9 +312,11 @@
     hidden = (x_ref[...].astype(F32) + projected).astype(BF16).astype(F32)
     hidden = [hidden[i * cells : (i + 1) * cells] for i in range(block)]
     acts = group_act(hidden, gn_ref[0:1])
+    first_fetch.wait()
     lines = conv_three(acts, one_ref, tile_rows, tile_cols)
     middle = per_frame([line + step_ref[...][None, :] for line in lines], block, tile_cols)
     acts = group_act(middle, gn_ref[1:2])
+    second_fetch.wait()
     lines = conv_three(acts, two_ref, tile_rows, tile_cols)
     moved = per_frame(lines, block, tile_cols)
     for i in range(block):
@@ -315,9 +327,15 @@
     return pl.pallas_call(
         functools.partial(residual, block, tile_rows, tile_cols),
         out_shape=jax.ShapeDtypeStruct(x.shape, BF16),
-        in_specs=[VMEM] * 7,
+        in_specs=[VMEM, VMEM, VMEM, VMEM, ANY, ANY, VMEM],
         out_specs=VMEM,
-        compiler_params=pltpu.CompilerParams(vmem_limit_bytes=60 * 2**20),
+        scratch_shapes=[
+            pltpu.VMEM(conv_one.shape, BF16),
+            pltpu.VMEM(conv_two.shape, BF16),
+            pltpu.SemaphoreType.DMA,
+            pltpu.SemaphoreType.DMA,
+        ],
+        compiler_params=pltpu.CompilerParams(vmem_limit_bytes=62 * 2**20),
     )(x, z, w_out, gn_gain, conv_one, conv_two, step)
 
 

time: 45.3 us -> 40 us (0.88)
  local copies, waits for them, and re-layouts: 4.81 us -> 0 us
    unnamed x12 -> x0, local copies, waits for them, and re-layouts: 4.81 us -> none
    pallas_call x1, Pallas kernels: 8.81 us -> 7.72 us  [resblock(): pl.pallas_call(functools.partial(residual, block, tile_rows, tile_cols),...]
    pallas_call x1, Pallas kernels: 31.4 us -> 32.1 us  [attention(): pl.pallas_call(functools.partial(attend, count), out_shape=jax.ShapeDtype...]
where the time goes in v3:
time: 40 us; the launch traced here: 39.8 us
  Pallas kernels  39.8 us (99%)
    pallas_call x1, Pallas kernels, attention(): pl.pallas_call(functools.partial(attend, count), out_shape=jax.ShapeDtype...  32.1 us
    pallas_call x1, Pallas kernels, resblock(): pl.pallas_call(functools.partial(residual, block, tile_rows, tile_cols),...  7.72 us

profile of v3, /device:TPU:0, one launch (start us, length us, event | category | flops | bytes accessed | tf_op | source)
XLA Modules:
  0.0 39.8 jit_solution(15400020537432170877)
XLA Ops:
  0.0 32.1 %shard_map.100 = bf16[3,4,16,8,128]{4,3,2,1,0:T(8,128)(2,1)} custom-call(bf16[4,16,8,320]{3,2,1,0:T(8,128)(2,1)} %bitcast.4, f32[320]{0:T(512)} %gain_ref.1, bf16[320,960]{1,0:T(8,128)(2,1)} %w_hbm.1, s32[16]{0:T(128)} %offsets_ref.1, s32[16]{0:T(128)} %numer_ref.1), custom_call_target="tpu_custom_call" | custom-call | tf_op jit(solution)/shard_map/pallas_call | solution.py:212
  32.1 7.7 %shard_map.101 = bf16[512,320]{1,0:T(8,128)(2,1)} custom-call(bf16[512,320]{1,0:T(8,128)(2,1)} %bitcast.5, bf16[3,512,128]{2,1,0:T(8,128)(2,1)} %bitcast.6, bf16[320,320]{1,0:T(8,128)(2,1)} %w_out_ref.1, f32[2,320]{1,0:T(2,128)} %gn_ref.1, bf16[3,3,320,320]{3,2,1,0:T(8,128)(2,1)} %one_hbm.1, bf16[3,3,320,320]{3,2,1,0:T(8,128)(2,1)} %two_hbm.1, f32[320]{0:T(512)} %step_ref.1), custom_call_target="tpu_custom_call" | custom-call | tf_op jit(solution)/shard_map/pallas_call | solution.py:327
